TPU v7x, 256 devices: a whole 4x4x8 slice. The times are simulated.
256 devices in a mesh: kx: 16 (over z, x_lo), ky: 4 (over x_hi, core), kz: 4 (over y).
Axes of the slice: x: 4 (x_hi: 2, x_lo: 2; x = x_hi * 2 + x_lo), y: 4, z: 8, core: 2. Of those that a mesh axis runs over, the one named last changes fastest.
Arguments:
- coefficients: bfloat16 [2, 16, 4, 4, 512, 2048], P(None, 'kx', 'ky', 'kz'), may hold values from -1 to 1
- shift_blocks: int32 [3], replicated, may hold values from 1 to 15, as said below
Outputs:
- centre: float32 [3, 512], replicated
- spread: float32 [3, 512], replicated
- coherence: float32 [3, 16, 4, 4], P(None, 'kx', 'ky', 'kz')
Inputs may be any that keep to these rules, and one draw needn't show every extreme that they name: The coefficients one period further along direction d are those of the first k-point of the string with plane-wave index g read at (g + 128 * shift_blocks[d]) mod 2048.
All inputs are finite; a program needn't handle non-finite values.
Results may differ from a plain program's by a relative error of at most 0.0003.
Values may be sent and summed in bfloat16 or wider, within the bound.
A program may use at most 128 MiB of HBM per device.

v0:
```python
import jax
import jax.numpy as jnp
from jax import lax
from jax.sharding import Mesh
from jax.sharding import PartitionSpec as P

KX = ("kx_0", "kx_1")
KY = ("ky_0", "ky_1")
KX_KY_KZ = ("kx_0", "kx_1", "ky_0", "ky_1", "kz")


def passed_along(value, axis, steps):
    count = lax.axis_size(axis)
    pairs = [(source, (source + steps) % count) for source in range(count)]
    return lax.ppermute(value, axis, pairs)


def one_axis_at_a_time(array, axes):
    for axis in axes:
        array = lax.psum(array, axis)
    return array


def pair_measure(own_point, partner):
    bands = own_point.shape[1]
    left_side = jnp.concatenate([own_point[0], own_point[1]], axis=1)
    right_side = jnp.concatenate(
        [
            jnp.concatenate([partner[0], partner[1]], axis=1),
            jnp.concatenate([partner[1], -partner[0]], axis=1),
        ],
        axis=0,
    )
    product = lax.dot_general(
        left_side, right_side, (((1,), (1,)), ((), ())), preferred_element_type=jnp.float32
    )
    real_part = product[:, :bands]
    imag_part = product[:, bands:]
    phases = jnp.arctan2(jnp.diagonal(imag_part), jnp.diagonal(real_part))
    coherence = jnp.sum(real_part * real_part + imag_part * imag_part) / bands
    return (phases, coherence)


def shards(coefficients, shift_blocks):
    planes = coefficients.shape[1]
    bands = coefficients.shape[4]
    width = coefficients.shape[5]
    own_planes = coefficients.reshape(2, planes, bands, width)
    shifts = shift_blocks * 128
    measure = jax.vmap(pair_measure, in_axes=(1, 1))
    next_first = passed_along(own_planes[:, 0], KX, -1)
    x_wrap = lax.axis_index(KX) == lax.axis_size(KX) - 1
    next_first = jnp.where(x_wrap, jnp.roll(next_first, -shifts[0], axis=-1), next_first)
    x_partner = jnp.concatenate([own_planes[:, 1:], next_first[:, None]], axis=1)
    x_phases, x_coherence = measure(own_planes, x_partner)
    earlier = passed_along(own_planes, KY, 1)
    y_wrap = lax.axis_index(KY) == 0
    y_partner = jnp.where(y_wrap, jnp.roll(own_planes, -shifts[1], axis=-1), own_planes)
    y_phases, y_earlier = measure(earlier, y_partner)
    y_coherence = passed_along(y_earlier, KY, -1)
    z_later = passed_along(own_planes, "kz", -1)
    z_wrap = lax.axis_index("kz") == lax.axis_size("kz") - 1
    z_partner = jnp.where(z_wrap, jnp.roll(z_later, -shifts[2], axis=-1), z_later)
    z_phases, z_coherence = measure(own_planes, z_partner)
    phases = jnp.stack([x_phases, y_phases, z_phases])
    coherence = jnp.stack([x_coherence, y_coherence, z_coherence]).reshape(3, planes, 1, 1)
    k_total = planes * lax.axis_size(KX) * lax.axis_size(KY) * lax.axis_size("kz")
    counts = jnp.array(
        [planes * lax.axis_size(KX), lax.axis_size(KY), lax.axis_size("kz")], jnp.float32
    )
    phase_sum = jnp.sum(phases, axis=1)
    totals, squares = (
        one_axis_at_a_time(phase_sum, KX_KY_KZ),
        one_axis_at_a_time(jnp.sum(phases * phases, axis=1), KX_KY_KZ),
    )
    mean_phase = totals / k_total
    variance = squares / k_total - mean_phase * mean_phase
    centre = -counts[:, None] * mean_phase / (2.0 * jnp.pi)
    spread = (counts[:, None] / (2.0 * jnp.pi)) ** 2 * variance
    return (centre, spread, coherence)


def solution(mesh):
    split = Mesh(
        mesh.devices.reshape(8, 2, 2, 2, mesh.shape["kz"]), ("kx_0", "kx_1", "ky_0", "ky_1", "kz")
    )
    in_specs = (P(None, KX, KY, "kz", None, None), P())
    out_specs = (P(), P(), P(None, KX, KY, "kz"))
    return jax.shard_map(
        shards, mesh=split, in_specs=in_specs, out_specs=out_specs, check_vma=False
    )
```

profile of v0, /device:TPU:1, one launch (start us, length us, event | category | flops | bytes accessed | tf_op | source)
XLA Modules:
  0.0 269.2 jit_solution(11188901696247821564)
XLA Ops:
  0.6 3.6 %collective-permute-start.2 = (bf16[2,1,512,2048]{3,2,0,1:T(8,128)(2,1)}, bf16[2,1,512,2048]{3,2,0,1:T(8,128)(2,1)}, u32[]{:S(2)}, u32[]{:S(2)}) collective-permute-start(bf16[2,1,512,2048]{3,2,0,1:T(8,128)(2,1)} %bitcast.97), channel_id=1, source_target_pairs={{0,3},{1,0},{2,1},{3,2},{4,7},{5,4},{6,5},{7,6},{8,11},{9,8},{10,9... | collective-permute-start | bytes 12582920 | tf_op jit(solution)/shard_map/ppermute | solution.py:15
  4.3 3.6 %collective-permute-start.1 = (bf16[2,1,512,2048]{3,2,0,1:T(8,128)(2,1)}, bf16[2,1,512,2048]{3,2,0,1:T(8,128)(2,1)}, u32[]{:S(2)}, u32[]{:S(2)}) collective-permute-start(bf16[2,1,512,2048]{3,2,0,1:T(8,128)(2,1)} %bitcast.98), channel_id=1, source_target_pairs={{0,4},{4,8},{8,12},{12,0},{1,5},{5,9},{9,13},{13,1},{2,6},{6,10},{... | collective-permute-start | bytes 12582920 | tf_op jit(solution)/shard_map/ppermute | solution.py:15
  7.8 5.6 %collective-permute-start = (bf16[2,512,2048]{2,1,0:T(8,128)(2,1)}, bf16[2,512,2048]{2,1,0:T(8,128)(2,1)}, u32[]{:S(2)}, u32[]{:S(2)}) collective-permute-start(bf16[2,512,2048]{2,1,0:T(8,128)(2,1)} %bitcast.99), channel_id=1, source_target_pairs={{0,240},{16,0},{32,16},{48,32},{64,48},{80,64},{96,80},{112,96},{1... | collective-permute-start | bytes 12582920 | tf_op jit(solution)/shard_map/ppermute | solution.py:15
  13.4 0.7 broadcast_multiply_fusion
  14.1 0.6 fusion.38
  17.4 6.5 %fusion.39 = bf16[2,1,512,2048]{3,2,1,0:T(8,128)(2,1)S(1)} fusion(bf16[2,1,512,2048]{3,2,0,1:T(8,128)(2,1)} %bitcast.100, s32[]{:T(128)S(6)} %select_n.67, pred[]{:T(512)S(6)} %eq.14), kind=kLoop, calls=%fused_computation.81 | loop fusion | flops 10485760 | bytes 8388613 | tf_op jit(solution)/shard_map/jit(_where)/select_n | solution.py:58
  23.9 0.0 copy-start
  23.9 1.5 fusion.35
  25.4 1.6 slice_bitcast_fusion.3
  26.9 0.5 copy-done
  27.4 4.2 %fusion.24 = bf16[2,1,512,2048]{3,2,0,1:T(8,128)(2,1)S(1)} fusion(bf16[2,1,512,2048]{3,2,0,1:T(8,128)(2,1)S(1)} %bitcast.101, s32[]{:T(128)S(6)} %select_n.67, pred[]{:T(512)S(6)} %eq.14), kind=kLoop, calls=%fused_computation.39 | loop fusion | flops 10485760 | bytes 8388613 | tf_op jit(solution)/shard_map/jit(_where)/select_n | solution.py:58
  31.7 1.5 slice_bitcast_fusion.2
  33.2 2.5 slice_bitcast_fusion.7
  35.7 58.1 %collective-permute-done.2 = bf16[2,1,512,2048]{3,2,0,1:T(8,128)(2,1)} collective-permute-done((bf16[2,1,512,2048]{3,2,0,1:T(8,128)(2,1)}, bf16[2,1,512,2048]{3,2,0,1:T(8,128)(2,1)}, u32[]{:S(2)}, u32[]{:S(2)}) %collective-permute-start.2) | collective-permute-done | bytes 4194336 | tf_op jit(solution)/shard_map/ppermute | solution.py:15
  93.8 6.5 %fusion.40 = bf16[2,1,512,2048]{3,2,1,0:T(8,128)(2,1)S(1)} fusion(bf16[2,1,512,2048]{3,2,0,1:T(8,128)(2,1)} %collective-permute-done.2, s32[]{:T(128)S(6)} %select_n.69, pred[]{:T(512)S(6)} %eq.15), kind=kLoop, calls=%fused_computation.82 | loop fusion | flops 10485760 | bytes 8388613 | tf_op jit(solution)/shard_map/jit(_where)/select_n | solution.py:63
  100.4 0.1 fusion.36
  100.5 0.1 slice_bitcast_fusion.1
  100.7 6.7 %fusion.22 = bf16[2,1,512,2048]{3,2,0,1:T(8,128)(2,1)S(1)} fusion(bf16[2,1,512,2048]{3,2,0,1:T(8,128)(2,1)} %collective-permute-done.2, s32[]{:T(128)S(6)} %select_n.69, pred[]{:T(512)S(6)} %eq.15), kind=kLoop, calls=%fused_computation.37 | loop fusion | flops 10485760 | bytes 8388613 | tf_op jit(solution)/shard_map/jit(_where)/select_n | solution.py:63
  107.4 0.1 slice_bitcast_fusion
  107.5 8.2 %fusion.29 = f32[1,512,1024]{2,1,0:T(8,128)} fusion(bf16[1,512,2048]{2,1,0:T(8,128)(2,1)S(1)} %fusion.36, bf16[1,512,2048]{2,1,0:T(8,128)(2,1)S(1)} %slice_bitcast_fusion, bf16[1,512,2048]{2,1,0:T(8,128)(2,1)S(1)} %slice_bitcast_fusion.1, bf16[1,512,2048]{2,1,0:T(8,128)(2,1)} %get-tuple-element.18, bf16[1,512,2048]{2,1,0:T(8,128)(2,1)} %get-tuple-element.17), kind=kOutput, calls=%fused_computation.54 | convolution fusion | flops 4336910336 | bytes 12582912 | tf_op jit(solution)/shard_map/vmap()/dot_general | solution.py:34
  115.7 2.5 add_reduce_fusion
  118.2 4.5 %gather_fusion.4 = f32[512]{0:T(512)S(1)} fusion(f32[512,512]{1,0:T(8,128)S(1)} %get-tuple-element.27, s32[512]{0:T(512)S(1)} %bitcast.91), kind=kCustom, calls=%fused_computation.4 | custom fusion | bytes 8192 | tf_op jit(solution)/shard_map/vmap(jit(diagonal))/cond/branch_0_fun/gather | solution.py:39
  122.7 4.5 %gather_fusion.5 = f32[512]{0:T(512)S(1)} fusion(f32[512,512]{1,0:T(8,128)S(1)} %get-tuple-element.26, s32[512]{0:T(512)S(1)} %bitcast.92), kind=kCustom, calls=%fused_computation.5 | custom fusion | bytes 8192 | tf_op jit(solution)/shard_map/vmap(jit(diagonal))/cond/branch_0_fun/gather | solution.py:39
  127.2 16.2 %collective-permute-done.1 = bf16[2,1,512,2048]{3,2,0,1:T(8,128)(2,1)} collective-permute-done((bf16[2,1,512,2048]{3,2,0,1:T(8,128)(2,1)}, bf16[2,1,512,2048]{3,2,0,1:T(8,128)(2,1)}, u32[]{:S(2)}, u32[]{:S(2)}) %collective-permute-start.1) | collective-permute-done | bytes 4194336 | tf_op jit(solution)/shard_map/ppermute | solution.py:15
  143.4 3.3 %slice_bitcast_fusion.5 = bf16[1,512,2048]{2,1,0:T(8,128)(2,1)} fusion(bf16[2,1,512,2048]{3,2,1,0:T(8,128)(2,1)} %bitcast.12), kind=kLoop, calls=%fused_computation.51 | loop fusion | bytes 4194304 | tf_op jit(solution)/shard_map/vmap()/squeeze;vmap()/transpose | solution.py:26
  146.7 3.2 %slice_bitcast_fusion.4 = bf16[1,512,2048]{2,1,0:T(8,128)(2,1)} fusion(bf16[2,1,512,2048]{3,2,0,1:T(8,128)(2,1)} %collective-permute-done.1), kind=kLoop, calls=%fused_computation.50 | loop fusion | bytes 4194304 | tf_op jit(solution)/shard_map/vmap()/squeeze;vmap()/transpose | solution.py:26
  150.0 0.0 copy-done.1
  150.0 0.0 copy-done.2
  150.0 0.0 copy-done.3
  150.0 8.1 %fusion.30 = f32[1,512,1024]{2,1,0:T(8,128)} fusion(bf16[1,512,2048]{2,1,0:T(8,128)(2,1)S(1)} %copy-done.1, bf16[1,512,2048]{2,1,0:T(8,128)(2,1)S(1)} %copy-done.3, bf16[1,512,2048]{2,1,0:T(8,128)(2,1)S(1)} %copy-done.2, bf16[1,512,2048]{2,1,0:T(8,128)(2,1)} %slice_bitcast_fusion.4, bf16[1,512,2048]{2,1,0:T(8,128)(2,1)} %slice_bitcast_fusion.5), kind=kOutput, calls=%fused_computation.55 | convolution fusion | flops 4336910336 | bytes 12582912 | tf_op jit(solution)/shard_map/vmap()/dot_general | solution.py:34
  158.1 2.5 add_reduce_fusion.1
  160.6 4.5 %gather_fusion.2 = f32[512]{0:T(512)S(1)} fusion(f32[512,512]{1,0:T(8,128)S(1)} %get-tuple-element.24, s32[512]{0:T(512)S(1)} %bitcast.93), kind=kCustom, calls=%fused_computation.2 | custom fusion | bytes 8192 | tf_op jit(solution)/shard_map/vmap(jit(diagonal))/cond/branch_0_fun/gather | solution.py:39
  165.1 4.5 %gather_fusion.3 = f32[512]{0:T(512)S(1)} fusion(f32[512,512]{1,0:T(8,128)S(1)} %get-tuple-element.23, s32[512]{0:T(512)S(1)} %bitcast.94), kind=kCustom, calls=%fused_computation.3 | custom fusion | bytes 8192 | tf_op jit(solution)/shard_map/vmap(jit(diagonal))/cond/branch_0_fun/gather | solution.py:39
  169.6 0.0 collective-permute-done
  169.6 7.9 %fusion.26 = bf16[2,512,2048]{2,1,0:T(8,128)(2,1)S(1)} fusion(bf16[2,512,2048]{2,1,0:T(8,128)(2,1)} %collective-permute-done, s32[]{:T(128)S(6)} %select_n.58, pred[]{:T(512)S(6)} %eq.13), kind=kLoop, calls=%fused_computation.41 | loop fusion | flops 10485760 | bytes 8388613 | tf_op jit(solution)/shard_map/jit(_where)/select_n | solution.py:53
  177.5 0.4 fusion.37
  177.9 8.1 %fusion.31 = f32[1,512,1024]{2,1,0:T(8,128)} fusion(bf16[1,512,2048]{2,1,0:T(8,128)(2,1)S(1)} %get-tuple-element.15, bf16[1,512,2048]{2,1,0:T(8,128)(2,1)S(1)} %get-tuple-element.16, bf16[1,512,2048]{2,1,0:T(8,128)(2,1)S(1)} %get-tuple-element.14, bf16[1,512,2048]{2,1,0:T(8,128)(2,1)} %get-tuple-element.18, bf16[1,512,2048]{2,1,0:T(8,128)(2,1)} %get-tuple-element.17), kind=kOutput, calls=%fused_computation.56 | convolution fusion | flops 4336910336 | bytes 12582912 | tf_op jit(solution)/shard_map/vmap()/dot_general | solution.py:34
  186.0 2.5 add_reduce_fusion.2
  188.6 4.5 %gather_fusion = f32[512]{0:T(512)S(1)} fusion(f32[512,512]{1,0:T(8,128)S(1)} %get-tuple-element.21, s32[512]{0:T(512)S(1)} %bitcast.95), kind=kCustom, calls=%fused_computation | custom fusion | bytes 8192 | tf_op jit(solution)/shard_map/vmap(jit(diagonal))/cond/branch_0_fun/gather | solution.py:39
  193.1 4.5 %gather_fusion.1 = f32[512]{0:T(512)S(1)} fusion(f32[512,512]{1,0:T(8,128)S(1)} %get-tuple-element.20, s32[512]{0:T(512)S(1)} %bitcast.96), kind=kCustom, calls=%fused_computation.1 | custom fusion | bytes 8192 | tf_op jit(solution)/shard_map/vmap(jit(diagonal))/cond/branch_0_fun/gather | solution.py:39
  198.9 2.4 collective-permute-start.3
  202.1 25.5 %all-reduce = (f32[3,512]{1,0:T(4,128)S(1)}, f32[3,512]{1,0:T(4,128)S(1)}) all-reduce(f32[3,512]{1,0:T(4,128)S(1)} %maximum_bitcast_fusion.23, f32[3,512]{1,0:T(4,128)S(1)} %maximum_multiply_fusion), channel_id=1, replica_groups=mesh['kx_0'=8,'kx_1'=2,'ky_0'=2,'ky_1'=2,'kz'=4] {'kx_0'}, use_global_device_ids=true, to_apply=%region_0.2 | all-reduce | flops 3072 | bytes 24576 | tf_op jit(solution)/shard_map/psum | solution.py:20
  227.7 5.0 %all-reduce.4 = (f32[3,512]{1,0:T(4,128)S(1)}, f32[3,512]{1,0:T(4,128)S(1)}) all-reduce(f32[3,512]{1,0:T(4,128)S(1)} %get-tuple-element.4, f32[3,512]{1,0:T(4,128)S(1)} %get-tuple-element.5), channel_id=1, replica_groups=mesh['kx_0'=8,'kx_1'=2,'ky_0'=2,'ky_1'=2,'kz'=4] {'kx_1'}, use_global_device_ids=true, to_apply=%region_1.3 | all-reduce | flops 3072 | bytes 24576 | tf_op jit(solution)/shard_map/psum | solution.py:20
  232.6 9.1 %all-reduce.3 = (f32[3,512]{1,0:T(4,128)S(1)}, f32[3,512]{1,0:T(4,128)S(1)}) all-reduce(f32[3,512]{1,0:T(4,128)S(1)} %get-tuple-element.12, f32[3,512]{1,0:T(4,128)S(1)} %get-tuple-element.13), channel_id=1, replica_groups=mesh['kx_0'=8,'kx_1'=2,'ky_0'=2,'ky_1'=2,'kz'=4] {'ky_0'}, use_global_device_ids=true, to_apply=%region_2.4 | all-reduce | flops 3072 | bytes 24576 | tf_op jit(solution)/shard_map/psum | solution.py:20
  241.7 14.5 %all-reduce.2 = (f32[3,512]{1,0:T(4,128)S(1)}, f32[3,512]{1,0:T(4,128)S(1)}) all-reduce(f32[3,512]{1,0:T(4,128)S(1)} %get-tuple-element.10, f32[3,512]{1,0:T(4,128)S(1)} %get-tuple-element.11), channel_id=1, replica_groups=mesh['kx_0'=8,'kx_1'=2,'ky_0'=2,'ky_1'=2,'kz'=4] {'ky_1'}, use_global_device_ids=true, to_apply=%region_3.5 | all-reduce | flops 3072 | bytes 24576 | tf_op jit(solution)/shard_map/psum | solution.py:20
  256.2 11.1 %all-reduce.1 = (f32[3,512]{1,0:T(4,128)S(1)}, f32[3,512]{1,0:T(4,128)S(1)}) all-reduce(f32[3,512]{1,0:T(4,128)S(1)} %get-tuple-element.8, f32[3,512]{1,0:T(4,128)S(1)} %get-tuple-element.9), channel_id=1, replica_groups=mesh['kx_0'=8,'kx_1'=2,'ky_0'=2,'ky_1'=2,'kz'=4] {'kz'}, use_global_device_ids=true, to_apply=%region_4.6 | all-reduce | flops 3072 | bytes 24576 | tf_op jit(solution)/shard_map/psum | solution.py:20
  267.3 0.7 subtract_multiply_fusion
  268.0 1.1 maximum_bitcast_fusion.24
  (14 shorter events, 0.2 us)
Async XLA Ops:
  0.6 93.2 %collective-permute-start.2 = (bf16[2,1,512,2048]{3,2,0,1:T(8,128)(2,1)}, bf16[2,1,512,2048]{3,2,0,1:T(8,128)(2,1)}, u32[]{:S(2)}, u32[]{:S(2)}) collective-permute-start(bf16[2,1,512,2048]{3,2,0,1:T(8,128)(2,1)} %bitcast.97), channel_id=1, source_target_pairs={{0,3},{1,0},{2,1},{3,2},{4,7},{5,4},{6,5},{7,6},{8,11},{9,8},{10,9... | collective-permute-start | bytes 12582920 | tf_op jit(solution)/shard_map/ppermute | solution.py:15
  4.3 139.2 %collective-permute-start.1 = (bf16[2,1,512,2048]{3,2,0,1:T(8,128)(2,1)}, bf16[2,1,512,2048]{3,2,0,1:T(8,128)(2,1)}, u32[]{:S(2)}, u32[]{:S(2)}) collective-permute-start(bf16[2,1,512,2048]{3,2,0,1:T(8,128)(2,1)} %bitcast.98), channel_id=1, source_target_pairs={{0,4},{4,8},{8,12},{12,0},{1,5},{5,9},{9,13},{13,1},{2,6},{6,10},{... | collective-permute-start | bytes 12582920 | tf_op jit(solution)/shard_map/ppermute | solution.py:15
  7.8 161.8 %collective-permute-start = (bf16[2,512,2048]{2,1,0:T(8,128)(2,1)}, bf16[2,512,2048]{2,1,0:T(8,128)(2,1)}, u32[]{:S(2)}, u32[]{:S(2)}) collective-permute-start(bf16[2,512,2048]{2,1,0:T(8,128)(2,1)} %bitcast.99), channel_id=1, source_target_pairs={{0,240},{16,0},{32,16},{48,32},{64,48},{80,64},{96,80},{112,96},{1... | collective-permute-start | bytes 12582920 | tf_op jit(solution)/shard_map/ppermute | solution.py:15
  23.9 3.6 %copy-start = (bf16[2,1,1,1,512,2048]{5,4,3,2,1,0:T(8,128)(2,1)S(1)}, bf16[2,1,1,1,512,2048]{5,4,3,2,1,0:T(8,128)(2,1)}, u32[]{:S(2)}) copy-start(bf16[2,1,1,1,512,2048]{5,4,3,2,1,0:T(8,128)(2,1)} %param.5) | copy-start | bytes 12582916
  143.4 6.5 %copy-start.1 = (bf16[1,512,2048]{2,1,0:T(8,128)(2,1)S(1)}, bf16[1,512,2048]{2,1,0:T(8,128)(2,1)}, u32[]{:S(2)}) copy-start(bf16[1,512,2048]{2,1,0:T(8,128)(2,1)} %fusion.35) | copy-start | bytes 6291460
  143.4 6.5 %copy-start.2 = (bf16[1,512,2048]{2,1,0:T(8,128)(2,1)S(1)}, bf16[1,512,2048]{2,1,0:T(8,128)(2,1)}, u32[]{:S(2)}) copy-start(bf16[1,512,2048]{2,1,0:T(8,128)(2,1)} %slice_bitcast_fusion.3) | copy-start | bytes 6291460
  143.4 6.5 %copy-start.3 = (bf16[1,512,2048]{2,1,0:T(8,128)(2,1)S(1)}, bf16[1,512,2048]{2,1,0:T(8,128)(2,1)}, u32[]{:S(2)}) copy-start(bf16[1,512,2048]{2,1,0:T(8,128)(2,1)} %slice_bitcast_fusion.2) | copy-start | bytes 6291460
  186.0 81.3 %copy-start.4 = (f32[3]{0:T(128)S(1)}, f32[3]{0:T(128)}, u32[]{:S(2)}) copy-start(f32[3]{0:T(128)} %constant.109) | copy-start | bytes 40
  186.0 81.3 %copy-start.5 = (f32[3]{0:T(128)S(1)}, f32[3]{0:T(128)}, u32[]{:S(2)}) copy-start(f32[3]{0:T(128)} %constant.106) | copy-start | bytes 40
  198.9 69.1 %collective-permute-start.3 = (f32[1]{0:T(128)}, f32[1]{0:T(128)}, u32[]{:S(2)}, u32[]{:S(2)}) collective-permute-start(f32[1]{0:T(128)} %bitcast.39), channel_id=1, source_target_pairs={{0,12},{4,0},{8,4},{12,8},{1,13},{5,1},{9,5},{13,9},{2,14},{6,2},{... | collective-permute-start | bytes 20 | tf_op jit(solution)/shard_map/ppermute | solution.py:15
where the time goes:
time: 271 us; the launch traced here: 269 us
  waiting for transfers between devices  74.3 us (27%)
  blocking collectives  65.2 us (24%)
  other arithmetic  43.9 us (16%)
  local copies, waits for them, and re-layouts  40.7 us (15%)
  matrix products  24.4 us (9%)
  starting transfers between devices  15.3 us (6%)
  between operations  5.43 us (2%)
    ppermute x4, waiting for transfers between devices, passed_along(): return lax.ppermute(value, axis, pairs)  74.3 us
    psum x5, blocking collectives, one_axis_at_a_time(): array = lax.psum(array, axis)  65.2 us
    gather x6, local copies, waits for them, and re-layouts, pair_measure(): phases = jnp.arctan2(jnp.diagonal(imag_part), jnp.diagonal(real_part))  27.1 us
    dot_general x3, matrix products, pair_measure(): lax.dot_general(left_side, right_side, (((1,), (1,)), ((), ())), preferre...  24.4 us
    ppermute x4, starting transfers between devices, passed_along(): return lax.ppermute(value, axis, pairs)  15.3 us
    select_n x2, other arithmetic, shards(): jnp.where(z_wrap, jnp.roll(z_later, -shifts[2], axis=-1), z_later)  13.3 us
    select_n x2, other arithmetic, shards(): jnp.where(y_wrap, jnp.roll(own_planes, -shifts[1], axis=-1), own_planes)  10.7 us
    transpose x3, local copies, waits for them, and re-layouts, pair_measure(): left_side = jnp.concatenate([own_point[0], own_point[1]], axis=1)  9 us
  transfers between devices with their start and end apart: 4, of which 2 were waited for; matrix products, arithmetic and copies ran while one was open for 29% of the time, Pallas kernels for 0%

commit v1 on v0

v1 whole, which is shorter than its diff:
```python
import functools

import jax
import jax.numpy as jnp
from jax import lax
from jax.experimental import pallas as pl
from jax.experimental.pallas import tpu as pltpu
from jax.sharding import PartitionSpec as P

SEND_ROWS = 32
STEP_ROWS = 64
HALF = 256
BLOCK = 128
TILE = 16
NT = (((1,), (1,)), ((), ()))


def kernel(
    nx, ny, nz,
    shift_ref, c_ref, out_ref, coh_ref,
    own, lhs1, lhs2, got, dre, dim, squares,
    plane, column, line,
    own_sem, send_a, send_y, send_fx, send_fz, recv,
    plane_send, plane_recv, column_send, column_recv, line_send, line_recv,
):
    kx, ky, kz = lax.axis_index("kx"), lax.axis_index("ky"), lax.axis_index("kz")
    bands, width = c_ref.shape[1], c_ref.shape[2]
    sends = bands // SEND_ROWS
    steps = bands // STEP_ROWS
    per_step = STEP_ROWS // SEND_ROWS
    half = min(HALF, bands)
    blocks = width // BLOCK
    levels = nx // 2
    xl, level = kx % 2, kx // 2
    core = ky % 2
    active = xl == core
    slot = xl * 4 + ky

    def device(x, y, z):
        return (x, y, z)

    def in_plane(index):
        return device(2 * level + index // 4, index % 4, kz)

    def in_column(index):
        return device(kx, ky, index)

    def in_line(index):
        return device(2 * index + xl, ky, kz)

    sibling = ky + 1 - 2 * core
    other_x = kx + 1 - 2 * xl
    up, down = (kz + 1) % nz, (kz + nz - 1) % nz

    barrier = pltpu.get_barrier_semaphore()
    peers = [in_plane((slot + step) % 8) for step in range(1, 8)]
    peers += [in_column((kz + step) % nz) for step in range(1, nz)]
    peers += [in_line((level + step) % levels) for step in range(1, levels)]
    peers += [device(kx, sibling, up), device(kx, sibling, down)]
    for peer in peers:
        pl.semaphore_signal(
            barrier, inc=1, device_id=peer, device_id_type=pl.DeviceIdType.MESH
        )
    load = pltpu.make_async_copy(c_ref, own, own_sem)
    load.start()
    pl.semaphore_wait(barrier, len(peers))

    def rows_of(index):
        return pl.ds(pl.multiple_of(index * SEND_ROWS, SEND_ROWS), SEND_ROWS)

    def remote(source, target_slot, index, send, target):
        return pltpu.make_async_remote_copy(
            src_ref=source.at[:, rows_of(index), :],
            dst_ref=got.at[target_slot, :, rows_of(index), :],
            send_sem=send.at[index],
            recv_sem=recv.at[target_slot, index],
            device_id=target,
            device_id_type=pl.DeviceIdType.MESH,
        )

    first_x = jnp.where(active, kx, other_x)
    first_y = jnp.where(active, sibling, ky)
    string_slot = jnp.where(active, 2, 1)
    string_y = jnp.where(active, sibling, ky)
    string_z = jnp.where(active, up, down)
    cross = device(other_x, 3 - ky, kz)
    along = device((kx + jnp.where(xl == 0, 2, nx - 2)) % nx, ky, kz)

    def to_first(index):
        return remote(c_ref, 0, index, send_a, device(first_x, first_y, kz))

    def to_string(index):
        return remote(c_ref, string_slot, index, send_y, device(kx, string_y, string_z))

    def to_cross(index):
        return remote(got.at[0], 2, index, send_fx, cross)

    def to_along(index):
        return remote(got.at[0], 1, index, send_fz, along)

    def arrived(edge, index):
        return pltpu.make_async_remote_copy(
            src_ref=got.at[edge, :, rows_of(index), :],
            dst_ref=got.at[edge, :, rows_of(index), :],
            send_sem=send_a.at[index],
            recv_sem=recv.at[edge, index],
            device_id=cross,
            device_id_type=pl.DeviceIdType.MESH,
        )

    def start_own(index, carry):
        to_first(index).start()
        to_string(index).start()
        return carry

    lax.fori_loop(0, sends, start_own, 0)

    dre[...] = jnp.zeros_like(dre)
    dim[...] = jnp.zeros_like(dim)
    squares[...] = jnp.zeros_like(squares)

    first_local = jnp.where(active, xl == 1, core == 1)
    second_local = jnp.logical_and(active, xl == 0)
    third_local = jnp.logical_or(jnp.logical_not(active), xl == 0)
    second_wrap = jnp.where(
        active, jnp.where(xl == 0, kx == 0, kx == nx - 1), kz == nz - 1
    )
    third_wrap = jnp.where(active, jnp.where(xl == 0, ky == 0, ky == ny - 1), kz == 0)
    chosen = active.astype(jnp.int32)
    second_shift = chosen * shift_ref[0] + (1 - chosen) * shift_ref[2]
    third_shift = chosen * shift_ref[1] + (1 - chosen) * shift_ref[2]

    def offset(shift, wrap, local):
        wrapped, kept = wrap.astype(jnp.int32), local.astype(jnp.int32)
        return wrapped * (kept * shift + (1 - kept) * (blocks - shift))

    second_offset = offset(second_shift, second_wrap, second_local)
    third_offset = offset(third_shift, third_wrap, third_local)

    def turn(source, target, amount):
        def body(tile, carry):
            rows = pl.ds(pl.multiple_of(tile * TILE, TILE), TILE)
            value = source[:, rows, :]
            reach = 1
            while reach < blocks:
                cut = reach * BLOCK
                moved = jnp.concatenate([value[:, :, cut:], value[:, :, :cut]], axis=2)
                value = jnp.where((amount // reach) % 2 == 1, moved, value)
                reach *= 2
            target[:, rows, :] = value
            return carry

        lax.fori_loop(0, bands // TILE, body, 0)

    load.wait()
    turn(own, lhs1, second_offset)

    @pl.when(active)
    def _():
        turn(own, lhs2, third_offset)

    @pl.when(jnp.logical_not(active))
    def _():
        def body(index, carry):
            arrived(0, index).wait_recv()
            return carry

        lax.fori_loop(0, sends, body, 0)
        turn(got.at[0], lhs2, third_offset)

    def product(edge, step, local, left):
        start = pl.multiple_of(step * STEP_ROWS, STEP_ROWS)
        right = got[edge, :, pl.ds(start, STEP_ROWS), :].reshape(2 * STEP_ROWS, width)
        for part in range(bands // half):
            columns = slice(part * half, (part + 1) * half)
            with_re = lax.dot_general(
                right, left[0, columns, :], NT, preferred_element_type=jnp.float32
            )
            with_im = lax.dot_general(
                right, left[1, columns, :], NT, preferred_element_type=jnp.float32
            )
            real = with_re[:STEP_ROWS] + with_im[STEP_ROWS:]
            imag = with_re[STEP_ROWS:] - with_im[:STEP_ROWS]
            norms = real * real + imag * imag
            squares[edge, :, :half] += norms.reshape(STEP_ROWS // 8, 8, half).sum(axis=0)
            row = lax.broadcasted_iota(jnp.int32, (STEP_ROWS, half), 0)
            column_id = lax.broadcasted_iota(jnp.int32, (STEP_ROWS, half), 1)
            on = column_id == row + (start - part * half)
            imag = jnp.where(local, with_im[:STEP_ROWS] - with_re[STEP_ROWS:], imag)
            dre[edge : edge + 1, columns] += jnp.sum(
                jnp.where(on, real, 0.0), axis=0, keepdims=True
            )
            dim[edge : edge + 1, columns] += jnp.sum(
                jnp.where(on, imag, 0.0), axis=0, keepdims=True
            )

    def trip(step, carry):
        @pl.when(step < steps)
        def _():
            @pl.when(active)
            def _():
                for inner in range(per_step):
                    index = step * per_step + inner
                    arrived(0, index).wait_recv()
                    to_cross(index).start()
                    to_along(index).start()

            product(0, step, first_local, own)

        @pl.when(step >= 1)
        def _():
            late = step - 1
            for inner in range(per_step):
                arrived(1, late * per_step + inner).wait_recv()
            product(1, late, second_local, lhs1)
            for inner in range(per_step):
                arrived(2, late * per_step + inner).wait_recv()
            product(2, late, third_local, lhs2)

        return carry

    lax.fori_loop(0, steps + 1, trip, 0)

    lane = lax.broadcasted_iota(jnp.int32, (1, bands), 1)
    found = jnp.zeros((1, bands), jnp.float32)
    for edge in range(3):
        total = jnp.sum(squares[edge], keepdims=True) / bands
        found = jnp.where(lane == 3 * slot + edge, total, found)
    phases = lax.atan2(dim[...], dre[...])
    plane[slot, 0:3, :] = phases[0:3]
    plane[slot, 6:7, :] = found

    def exchange(buffer, me, count, place, send, receive):
        copies = []
        for step in range(1, count):
            copies.append(
                pltpu.make_async_remote_copy(
                    src_ref=buffer.at[me],
                    dst_ref=buffer.at[me],
                    send_sem=send.at[step],
                    recv_sem=receive.at[me],
                    device_id=place((me + step) % count),
                    device_id_type=pl.DeviceIdType.MESH,
                )
            )
        for copy in copies:
            copy.start()
        for step in range(1, count):
            source = (me + step) % count
            pltpu.make_async_remote_copy(
                src_ref=buffer.at[source],
                dst_ref=buffer.at[source],
                send_sem=send.at[step],
                recv_sem=receive.at[source],
                device_id=place(source),
                device_id_type=pl.DeviceIdType.MESH,
            ).wait_recv()
        return copies

    copies = exchange(plane, slot, 8, in_plane, plane_send, plane_recv)
    groups = [[], [], []]
    for index in range(8):
        if index // 4 == index % 2:
            groups[0] += [plane[index, 0:1, :], plane[index, 1:2, :]]
            groups[1] += [plane[index, 2:3, :]]
        else:
            groups[1] += [plane[index, 0:1, :]]
            groups[2] += [plane[index, 1:2, :], plane[index, 2:3, :]]
    for direction in range(3):
        mean = sum(groups[direction]) / 8.0
        spreads = sum((value - mean) * (value - mean) for value in groups[direction])
        column[kz, direction : direction + 1, :] = mean
        column[kz, 3 + direction : 4 + direction, :] = spreads
    plane_found = sum(plane[index, 6:7, :] for index in range(8))
    column[kz, 6:7, :] = plane_found

    copies += exchange(column, kz, nz, in_column, column_send, column_recv)

    def merged(buffer, count, weight):
        mean = sum(buffer[index, 0:3, :] for index in range(count)) / float(count)
        spreads = sum(buffer[index, 3:6, :] for index in range(count))
        for index in range(count):
            off = buffer[index, 0:3, :] - mean
            spreads = spreads + weight * (off * off)
        return mean, spreads

    mean, spreads = merged(column, nz, 8.0)
    line[level, 0:3, :] = mean
    line[level, 3:6, :] = spreads
    line[level, 6:7, :] = plane_found
    copies += exchange(line, level, levels, in_line, line_send, line_recv)
    mean, spreads = merged(line, levels, 8.0 * nz)

    which = lax.broadcasted_iota(jnp.int32, (3, bands), 0)
    count = jnp.where(which == 0, float(nx), jnp.where(which == 1, float(ny), float(nz)))
    scale = count / (2.0 * jnp.pi)
    out_ref[0:3, :] = -count * mean / (2.0 * jnp.pi)
    out_ref[3:6, :] = scale * scale * (spreads / (nx * ny * nz))

    above = column[up, 6:7, :]
    ahead = line[(level + 1) % levels, 6:7, :]
    x_from = jnp.where(xl == 0, 3 * (core * 4 + ky), 3 * (core * 4 + ky) + 1)
    x_far = jnp.logical_and(xl == 1, core == 0)
    x_row = jnp.where(x_far, ahead, plane_found)
    y_even = 3 * (xl * 4 + (ky // 2) * 2 + 1 - xl)
    y_odd = jnp.where(xl == 1, 3 * slot + 2, 3 * ((ky + 1) % ny) + 2)
    y_from = jnp.where(core == 0, y_even, y_odd)
    z_from = jnp.where(active, 3 * (xl * 4 + sibling) + 2, 3 * slot + 1)
    z_row = jnp.where(active, above, plane_found)
    for direction, (row, place) in enumerate(
        ((x_row, x_from), (plane_found, y_from), (z_row, z_from))
    ):
        value = jnp.sum(jnp.where(lane == place, row, 0.0), axis=1, keepdims=True)
        coh_ref[direction : direction + 1, :] = jnp.broadcast_to(value, (1, 128))

    for copy in copies:
        copy.wait_send()

    def finish(index, carry):
        to_first(index).wait_send()
        to_string(index).wait_send()

        @pl.when(active)
        def _():
            to_cross(index).wait_send()
            to_along(index).wait_send()

        return carry

    lax.fori_loop(0, sends, finish, 0)


def solution(mesh):
    nx, ny, nz = mesh.shape["kx"], mesh.shape["ky"], mesh.shape["kz"]
    levels = nx // 2

    def shards(coefficients, shift_blocks):
        bands, width = coefficients.shape[4], coefficients.shape[5]
        own = coefficients.reshape(2, bands, width)
        sends = bands // SEND_ROWS
        dma = pltpu.SemaphoreType.DMA
        out, coherence = pl.pallas_call(
            functools.partial(kernel, nx, ny, nz),
            out_shape=(
                jax.ShapeDtypeStruct((6, bands), jnp.float32),
                jax.ShapeDtypeStruct((3, 128), jnp.float32),
            ),
            in_specs=[
                pl.BlockSpec(memory_space=pltpu.SMEM),
                pl.BlockSpec(memory_space=pl.ANY),
            ],
            out_specs=(
                pl.BlockSpec(memory_space=pltpu.VMEM),
                pl.BlockSpec(memory_space=pltpu.VMEM),
            ),
            scratch_shapes=[
                pltpu.VMEM((2, bands, width), jnp.bfloat16),
                pltpu.VMEM((2, bands, width), jnp.bfloat16),
                pltpu.VMEM((2, bands, width), jnp.bfloat16),
                pltpu.VMEM((3, 2, bands, width), jnp.bfloat16),
                pltpu.VMEM((8, bands), jnp.float32),
                pltpu.VMEM((8, bands), jnp.float32),
                pltpu.VMEM((3, 8, min(HALF, bands)), jnp.float32),
                pltpu.VMEM((8, 8, bands), jnp.float32),
                pltpu.VMEM((nz, 8, bands), jnp.float32),
                pltpu.VMEM((levels, 8, bands), jnp.float32),
                dma(()),
                dma((sends,)), dma((sends,)), dma((sends,)), dma((sends,)),
                dma((3, sends)),
                dma((8,)), dma((8,)),
                dma((nz,)), dma((nz,)),
                dma((levels,)), dma((levels,)),
            ],
            compiler_params=pltpu.CompilerParams(
                collective_id=0,
                has_side_effects=True,
                vmem_limit_bytes=60 * 1024 * 1024,
            ),
        )(shift_blocks, own)
        return out[0:3], out[3:6], coherence[:, 0:1].reshape(3, 1, 1, 1)

    return jax.shard_map(
        shards,
        mesh=mesh,
        in_specs=(P(None, "kx", "ky", "kz", None, None), P()),
        out_specs=(P(), P(), P(None, "kx", "ky", "kz")),
        check_vma=False,
    )
```

time: 271 us -> 87.9 us (0.32)
  Pallas kernels: 0 us -> 84.3 us
  waiting for transfers between devices: 74.3 us -> 0 us
  blocking collectives: 65.2 us -> 0 us
  other arithmetic: 43.9 us -> 0 us
  local copies, waits for them, and re-layouts: 40.7 us -> 2.7 us
  matrix products: 24.4 us -> 0 us
  starting transfers between devices: 15.3 us -> 0 us
  between operations: 5.43 us -> 0.64 us
    pallas_call x0 -> x1, Pallas kernels: none -> 84.3 us  [shards(): pl.pallas_call(functools.partial(kernel, nx, ny, nz), out_shape=(jax.Shap...]
    ppermute x4 -> x0, waiting for transfers between devices: 74.3 us -> none  [passed_along(): return lax.ppermute(value, axis, pairs)]
    psum x5 -> x0, blocking collectives: 65.2 us -> none  [one_axis_at_a_time(): array = lax.psum(array, axis)]
    select_n x5 -> x0, other arithmetic: 31.8 us -> none  [the longest x2 13.3 us: shards(): jnp.where(z_wrap, jnp.roll(z_later, -shifts[2], axis=-1), z_later)]
    gather x6 -> x0, local copies, waits for them, and re-layouts: 27.1 us -> none  [pair_measure(): phases = jnp.arctan2(jnp.diagonal(imag_part), jnp.diagonal(real_part))]
    dot_general x3 -> x0, matrix products: 24.4 us -> none  [pair_measure(): lax.dot_general(left_side, right_side, (((1,), (1,)), ((), ())), preferre...]
    ppermute x4 -> x0, starting transfers between devices: 15.3 us -> none  [passed_along(): return lax.ppermute(value, axis, pairs)]
    transpose x7 -> x0, local copies, waits for them, and re-layouts: 12.4 us -> none  [the longest x3 9 us: pair_measure(): left_side = jnp.concatenate([own_point[0], own_point[1]], axis=1)]
  transfers between devices with their start and end apart: 4 -> 0, of which waited for: 2 -> 0; matrix products, arithmetic and copies ran while one was open for 29% -> 0% of each run, Pallas kernels for 0% -> 0%
where the time goes in v1:
time: 87.9 us; the launch traced here: 87.6 us
  Pallas kernels  84.3 us (96%)
  local copies, waits for them, and re-layouts  2.7 us (3%)
    pallas_call x1, Pallas kernels, shards(): pl.pallas_call(functools.partial(kernel, nx, ny, nz), out_shape=(jax.Shap...  84.3 us
    slice x2, local copies, waits for them, and re-layouts, shards(): return (out[0:3], out[3:6], coherence[:, 0:1].reshape(3, 1, 1, 1))  2.7 us

profile of v1, /device:TPU:1, one launch (start us, length us, event | category | flops | bytes accessed | tf_op | source)
XLA Modules:
  0.0 87.6 jit_solution(7589611454951207709)
XLA Ops:
  0.6 84.3 %shard_map.49 = (f32[6,512]{1,0:T(8,128)}, f32[3,128]{1,0:T(4,128)}) custom-call(s32[3]{0:T(128)} %shift_ref.1, bf16[2,512,2048]{2,1,0:T(8,128)(2,1)} %bitcast.2), custom_call_target="tpu_custom_call" | custom-call | tf_op jit(solution)/shard_map/pallas_call | solution.py:342
  84.9 1.4 %fusion = (f32[3,512]{1,0:T(4,128)}, f32[3,512]{1,0:T(4,128)}) fusion(f32[6,512]{1,0:T(8,128)} %get-tuple-element.5), kind=kLoop, calls=%fused_computation.1 | loop fusion | bytes 24576 | tf_op jit(solution)/shard_map/slice | solution.py:380
  86.3 1.3 %slice_reduce_fusion = f32[3]{0:T(128)} fusion(f32[3,128]{1,0:T(4,128)} %get-tuple-element.6), kind=kLoop, calls=%fused_computation | loop fusion | bytes 24 | tf_op jit(solution)/shard_map/slice | solution.py:380

commit v2 on v1

v2 whole, which is shorter than its diff:
```python
import functools

import jax
import jax.numpy as jnp
from jax import lax
from jax.experimental import pallas as pl
from jax.experimental.pallas import tpu as pltpu
from jax.sharding import PartitionSpec as P

SEND_ROWS = 16
STEP_ROWS = 64
HALF = 256
BLOCK = 128
TILE = 16
AHEAD = 12
LAST = 128
FIRST = 64
NN = (((1,), (0,)), ((), ()))
MESH = pl.DeviceIdType.MESH


def kernel(
    nx, ny, nz,
    shift_hbm, c_ref, out_ref,
    shift_ref, result, own, turned, left, got, dre, dim, squares,
    plane_a, column_a, line_a, sheet_b, line_b,
    shift_sem, own_sem, out_sem, send_a, send_y, send_fx, send_fz, recv,
    plane_send, plane_recv, column_send, column_recv, line_send, line_recv,
    sheet_send, sheet_recv,
    second_ring, third_ring,
):
    kx, ky, kz = lax.axis_index("kx"), lax.axis_index("ky"), lax.axis_index("kz")
    bands, width = c_ref.shape[1], c_ref.shape[2]
    sends = bands // SEND_ROWS
    steps = bands // STEP_ROWS
    per_step = STEP_ROWS // SEND_ROWS
    blocks = width // BLOCK
    early = bands - LAST
    levels = nx // 2
    xl, level = kx % 2, kx // 2
    core = ky % 2
    active = xl == core
    slot = xl * 4 + ky

    def device(x, y, z):
        return (x, y, z)

    def in_plane(index):
        return device(2 * level + index // 4, index % 4, kz)

    def in_column(index):
        return device(kx, ky, index)

    def in_line(index):
        return device(2 * index + xl, ky, kz)

    sibling = ky + 1 - 2 * core
    other_x = kx + 1 - 2 * xl
    up, down = (kz + 1) % nz, (kz + nz - 1) % nz

    def signal(semaphore, peers):
        for peer in peers:
            pl.semaphore_signal(semaphore, inc=1, device_id=peer, device_id_type=MESH)

    barrier = pltpu.get_barrier_semaphore()
    beside = [in_column(up), in_column(down)]
    beside += [in_line((level + 1) % levels), in_line((level + levels - 1) % levels)]
    near = beside + [device(kx, sibling, up), device(kx, sibling, down)]
    near += [in_plane((slot + step) % 8) for step in range(1, 8)]
    next_but_one = [
        in_line((level + 2) % levels), in_line((level + levels - 2) % levels)
    ]
    signal(barrier, near)
    loads = [
        pltpu.make_async_copy(c_ref.at[:, rows, :], own.at[:, rows, :], own_sem.at[index])
        for index, rows in enumerate((pl.ds(0, FIRST), pl.ds(FIRST, bands - FIRST)))
    ]
    shift_load = pltpu.make_async_copy(shift_hbm, shift_ref, shift_sem)
    for load in loads + [shift_load]:
        load.start()
    pl.semaphore_wait(barrier, len(near))

    def rows_of(index):
        return pl.ds(pl.multiple_of(index * SEND_ROWS, SEND_ROWS), SEND_ROWS)

    def remote(source, target_slot, index, send, target):
        return pltpu.make_async_remote_copy(
            src_ref=source.at[:, rows_of(index), :],
            dst_ref=got.at[target_slot, :, rows_of(index), :],
            send_sem=send.at[index],
            recv_sem=recv.at[target_slot, index],
            device_id=target,
            device_id_type=MESH,
        )

    first_x = jnp.where(active, kx, other_x)
    first_y = jnp.where(active, sibling, ky)
    string_slot = jnp.where(active, 2, 1)
    string_y = jnp.where(active, sibling, ky)
    string_z = jnp.where(active, up, down)
    cross = device(other_x, 3 - ky, kz)
    along = device((kx + jnp.where(xl == 0, 2, nx - 2)) % nx, ky, kz)

    def to_first(index):
        return remote(own, 0, index, send_a, device(first_x, first_y, kz))

    def to_string(index):
        return remote(own, string_slot, index, send_y, device(kx, string_y, string_z))

    def to_cross(index):
        return remote(got.at[0], 2, index, send_fx, cross)

    def to_along(index):
        return remote(got.at[0], 1, index, send_fz, along)

    def arrived(edge, index):
        return pltpu.make_async_remote_copy(
            src_ref=got.at[edge, :, rows_of(index), :],
            dst_ref=got.at[edge, :, rows_of(index), :],
            send_sem=send_a.at[index],
            recv_sem=recv.at[edge, index],
            device_id=cross,
            device_id_type=MESH,
        )

    def start_own(index, carry):
        to_first(index).start()
        to_string(index).start()
        return carry

    loads[0].wait()
    lax.fori_loop(0, FIRST // SEND_ROWS, start_own, 0)
    signal(second_ring, beside)
    shift_load.wait()
    dre[...] = jnp.zeros_like(dre)
    dim[...] = jnp.zeros_like(dim)
    squares[...] = jnp.zeros_like(squares)

    first_local = jnp.where(active, xl == 1, core == 1)
    second_local = jnp.logical_and(active, xl == 0)
    third_local = jnp.logical_or(jnp.logical_not(active), xl == 0)
    second_wrap = jnp.where(
        active, jnp.where(xl == 0, kx == 0, kx == nx - 1), kz == nz - 1
    )
    third_wrap = jnp.where(active, jnp.where(xl == 0, ky == 0, ky == ny - 1), kz == 0)
    chosen = active.astype(jnp.int32)
    second_shift = chosen * shift_ref[0] + (1 - chosen) * shift_ref[2]
    third_shift = chosen * shift_ref[1] + (1 - chosen) * shift_ref[2]

    def offset(shift, wrap, local):
        wrapped, kept = wrap.astype(jnp.int32), local.astype(jnp.int32)
        return wrapped * (kept * shift + (1 - kept) * (blocks - shift))

    second_offset = offset(second_shift, second_wrap, second_local)
    third_offset = offset(third_shift, third_wrap, third_local)

    def turn(source, amount, piece, pieces):
        def body(tile, carry):
            rows = pl.ds(pl.multiple_of(tile * TILE, TILE), TILE)
            value = source[:, rows, :]
            reach = 1
            while reach < blocks:
                cut = reach * BLOCK
                moved = jnp.concatenate([value[:, :, cut:], value[:, :, :cut]], axis=2)
                value = jnp.where((amount // reach) % 2 == 1, moved, value)
                reach *= 2
            turned[:, rows, :] = value
            return carry

        share = bands // TILE // pieces
        lax.fori_loop(piece * share, (piece + 1) * share, body, 0)

    def transpose(source, edge, piece, pieces):
        def body(index, carry):
            part, block = index // blocks, index % blocks
            at = pl.ds(pl.multiple_of(block * BLOCK, BLOCK), BLOCK)
            left[edge, part, at, :] = source[part, :, at].T
            return carry

        share = 2 * blocks // pieces
        lax.fori_loop(piece * share, (piece + 1) * share, body, 0)

    def pass_on(index):
        arrived(0, index).wait_recv()
        to_cross(index).start()
        to_along(index).start()

    def while_passing(first, count, work):
        def body(piece, carry):
            @pl.when(active)
            def _():
                pass_on(first + piece)

            work(piece)
            return carry

        lax.fori_loop(0, count, body, 0)

    def third_source(piece):
        @pl.when(active)
        def _():
            turn(own, third_offset, piece, 2)

        @pl.when(jnp.logical_not(active))
        def _():
            turn(got.at[0], third_offset, piece, 2)

    loads[1].wait()
    lax.fori_loop(FIRST // SEND_ROWS, sends, start_own, 0)
    transpose(own, 0, 0, 1)
    pl.semaphore_wait(second_ring, len(beside))
    signal(third_ring, beside[0:2] + next_but_one)
    while_passing(0, 2, lambda piece: turn(own, second_offset, piece, 2))
    while_passing(2, 4, lambda piece: transpose(turned, 1, piece, 4))

    @pl.when(jnp.logical_not(active))
    def _():
        def body(index, carry):
            arrived(0, index).wait_recv()
            return carry

        lax.fori_loop(0, sends, body, 0)

    while_passing(6, 2, third_source)
    while_passing(8, 4, lambda piece: transpose(turned, 2, piece, 4))

    def product(edge, step, local):
        start = pl.multiple_of(step * STEP_ROWS, STEP_ROWS)
        right = got[edge, :, pl.ds(start, STEP_ROWS), :].reshape(2 * STEP_ROWS, width)
        for part in range(bands // HALF):
            columns = slice(part * HALF, (part + 1) * HALF)
            with_re = lax.dot_general(
                right, left[edge, 0, :, columns], NN, preferred_element_type=jnp.float32
            )
            with_im = lax.dot_general(
                right, left[edge, 1, :, columns], NN, preferred_element_type=jnp.float32
            )
            real = with_re[:STEP_ROWS] + with_im[STEP_ROWS:]
            imag = with_re[STEP_ROWS:] - with_im[:STEP_ROWS]
            norms = real * real + imag * imag
            squares[edge] += norms.reshape(STEP_ROWS // 8, 8, HALF).sum(axis=0)
            row = lax.broadcasted_iota(jnp.int32, (STEP_ROWS, HALF), 0)
            column_id = lax.broadcasted_iota(jnp.int32, (STEP_ROWS, HALF), 1)
            on = column_id == row + (start - part * HALF)
            imag = jnp.where(local, with_im[:STEP_ROWS] - with_re[STEP_ROWS:], imag)
            dre[edge : edge + 1, columns] += jnp.sum(
                jnp.where(on, real, 0.0), axis=0, keepdims=True
            )
            dim[edge : edge + 1, columns] += jnp.sum(
                jnp.where(on, imag, 0.0), axis=0, keepdims=True
            )

    def copy_of(buffer, part, me, target, count, place, send, receive, step):
        return pltpu.make_async_remote_copy(
            src_ref=buffer.at[me],
            dst_ref=buffer.at[me],
            send_sem=send.at[part, step],
            recv_sem=receive.at[part, me],
            device_id=place(target),
            device_id_type=MESH,
        )

    planes = (slot, 8, in_plane, plane_send, plane_recv)
    columns_y = (kz, nz, in_column, column_send, column_recv)
    lines = (level, levels, in_line, line_send, line_recv)

    def start_exchange(buffer, part, group):
        me, count, place, send, receive = group
        for step in range(1, count):
            target = (me + step) % count
            copy_of(buffer, part, me, target, count, place, send, receive, step).start()

    def await_exchange(buffer, part, group):
        me, count, place, send, receive = group
        for step in range(1, count):
            other = (me + step) % count
            copy_of(buffer, part, other, other, count, place, send, receive, step).wait_recv()

    def drain_exchange(buffer, part, group):
        me, count, place, send, receive = group
        for step in range(1, count):
            target = (me + step) % count
            copy_of(buffer, part, me, target, count, place, send, receive, step).wait_send()

    def plane_means(plane, column):
        groups = [[], [], []]
        for index in range(8):
            rows = [plane[index, edge : edge + 1, :] for edge in range(3)]
            if index // 4 == index % 2:
                groups[0] += rows[0:2]
                groups[1] += rows[2:3]
            else:
                groups[1] += rows[0:1]
                groups[2] += rows[1:3]
        for direction in range(3):
            mean = sum(groups[direction]) / 8.0
            spreads = sum((value - mean) * (value - mean) for value in groups[direction])
            column[kz, direction : direction + 1, :] = mean
            column[kz, 3 + direction : 4 + direction, :] = spreads

    def merged(buffer, count, weight):
        mean = sum(buffer[index, 0:3, :] for index in range(count)) / float(count)
        spreads = sum(buffer[index, 3:6, :] for index in range(count))
        for index in range(count):
            off = buffer[index, 0:3, :] - mean
            spreads = spreads + weight * (off * off)
        return mean, spreads

    def column_means(column, line):
        mean, spreads = merged(column, nz, 8.0)
        line[level, 0:3, :] = mean
        line[level, 3:6, :] = spreads

    def results(line, where):
        mean, spreads = merged(line, levels, 8.0 * nz)
        which = lax.broadcasted_iota(jnp.int32, mean.shape, 0)
        count = jnp.where(
            which == 0, float(nx), jnp.where(which == 1, float(ny), float(nz))
        )
        scale = count / (2.0 * jnp.pi)
        result[0:3, where] = -count * mean / (2.0 * jnp.pi)
        result[3:6, where] = scale * scale * (spreads / (nx * ny * nz))

    def write(where, index):
        return pltpu.make_async_copy(
            result.at[:, where], out_ref.at[:, where], out_sem.at[index]
        )

    def sheet_copy(plane_at, y_at, place, step):
        return pltpu.make_async_remote_copy(
            src_ref=sheet_b.at[y_at, plane_at],
            dst_ref=sheet_b.at[y_at, plane_at],
            send_sem=sheet_send.at[step],
            recv_sem=sheet_recv.at[y_at, plane_at],
            device_id=place,
            device_id_type=MESH,
        )

    def sheet_peers():
        for shift in range(nz):
            for step in range(8):
                if shift or step:
                    to_plane, to_y = (slot + step) % 8, (kz + shift) % nz
                    place = device(2 * level + to_plane // 4, to_plane % 4, to_y)
                    yield shift * 8 + step, to_plane, to_y, place

    def sheet_means():
        parts = [[], []]
        for y_at in range(nz):
            for index in range(8):
                parts[index // 4 != index % 2].append(sheet_b[y_at, index, 0:3, :])
        number = float(8 * nz)
        one, two = sum(parts[0]), sum(parts[1])
        means = [
            (one[0:1] + one[1:2]) / number,
            (one[2:3] + two[0:1]) / number,
            (two[1:2] + two[2:3]) / number,
        ]
        centre_one = jnp.concatenate([means[0], means[0], means[1]], axis=0)
        centre_two = jnp.concatenate([means[1], means[2], means[2]], axis=0)
        one = sum((value - centre_one) * (value - centre_one) for value in parts[0])
        two = sum((value - centre_two) * (value - centre_two) for value in parts[1])
        line_b[level, 0:3, :] = jnp.concatenate(means, axis=0)
        line_b[level, 3:4, :] = one[0:1] + one[1:2]
        line_b[level, 4:5, :] = one[2:3] + two[0:1]
        line_b[level, 5:6, :] = two[1:2] + two[2:3]

    def finish_rows(edge, step, local):
        for inner in range(per_step):
            arrived(edge, step * per_step + inner).wait_recv()
        product(edge, step, local)

    def trip(step, carry):
        few = step < 4

        def maybe_pass(place):
            index = jnp.where(
                few, AHEAD + 2 * step + place // 2, AHEAD + 8 + 4 * (step - 4) + place
            )
            due = jnp.logical_or(
                jnp.logical_and(few, place % 2 == 0),
                jnp.logical_and(jnp.logical_not(few), step < steps - 1),
            )

            @pl.when(jnp.logical_and(active, due))
            def _():
                pass_on(index)

        def follow(edge, local):
            @pl.when(step >= 1)
            def _():
                finish_rows(edge, step - 1, local)

        @pl.when(step == steps - 1)
        def _():
            phases = lax.atan2(dim[:, 0:early], dre[:, 0:early])
            plane_a[slot, 0:3, :] = phases[0:3]
            start_exchange(plane_a, 0, planes)

        maybe_pass(0)
        product(0, step, first_local)
        maybe_pass(1)
        follow(1, second_local)
        maybe_pass(2)
        follow(2, third_local)
        maybe_pass(3)
        return carry

    lax.fori_loop(0, steps, trip, 0)
    finish_rows(1, steps - 1, second_local)
    finish_rows(2, steps - 1, third_local)

    lane = lax.broadcasted_iota(jnp.int32, (1, LAST), 1)
    found = jnp.zeros((1, LAST), jnp.float32)
    for edge in range(3):
        total = jnp.sum(squares[edge], keepdims=True) / bands
        found = jnp.where(lane == 3 * slot + edge, total, found)
    phases = lax.atan2(dim[:, early:bands], dre[:, early:bands])
    sheet_b[kz, slot, 0:3, :] = phases[0:3]
    sheet_b[kz, slot, 3:4, :] = found
    pl.semaphore_wait(third_ring, 2 + len(next_but_one))
    for step, _, _, place in sheet_peers():
        sheet_copy(slot, kz, place, step).start()

    await_exchange(plane_a, 0, planes)
    plane_means(plane_a, column_a)
    start_exchange(column_a, 0, columns_y)

    for step, from_plane, from_y, place in sheet_peers():
        sheet_copy(from_plane, from_y, place, step).wait_recv()
    sheet_means()
    plane_found = sum(sheet_b[kz, index, 3:4, :] for index in range(8))
    above = sum(sheet_b[up, index, 3:4, :] for index in range(8))
    line_b[level, 6:7, :] = plane_found
    start_exchange(line_b, 1, lines)

    await_exchange(column_a, 0, columns_y)
    column_means(column_a, line_a)
    start_exchange(line_a, 0, lines)
    drain_exchange(plane_a, 0, planes)
    drain_exchange(column_a, 0, columns_y)
    for step, _, _, place in sheet_peers():
        sheet_copy(slot, kz, place, step).wait_send()

    def finish(index, carry):
        to_first(index).wait_send()
        to_string(index).wait_send()

        @pl.when(active)
        def _():
            to_cross(index).wait_send()
            to_along(index).wait_send()

        return carry

    lax.fori_loop(0, sends, finish, 0)

    await_exchange(line_b, 1, lines)
    results(line_b, slice(early, bands))
    ahead = line_b[(level + 1) % levels, 6:7, :]
    x_from = jnp.where(xl == 0, 3 * (core * 4 + ky), 3 * (core * 4 + ky) + 1)
    x_far = jnp.logical_and(xl == 1, core == 0)
    x_row = jnp.where(x_far, ahead, plane_found)
    y_even = 3 * (xl * 4 + (ky // 2) * 2 + 1 - xl)
    y_odd = jnp.where(xl == 1, 3 * slot + 2, 3 * ((ky + 1) % ny) + 2)
    y_from = jnp.where(core == 0, y_even, y_odd)
    z_from = jnp.where(active, 3 * (xl * 4 + sibling) + 2, 3 * slot + 1)
    z_row = jnp.where(active, above, plane_found)
    coherences = jnp.zeros((1, LAST), jnp.float32)
    for direction, (row, place) in enumerate(
        ((x_row, x_from), (plane_found, y_from), (z_row, z_from))
    ):
        value = jnp.sum(jnp.where(lane == place, row, 0.0), axis=1, keepdims=True)
        coherences = jnp.where(lane == direction, value, coherences)
    result[6:7, early:bands] = coherences
    write(pl.ds(early, LAST), 1).start()
    await_exchange(line_a, 0, lines)
    results(line_a, slice(0, early))
    write(pl.ds(0, early), 0).start()
    drain_exchange(line_a, 0, lines)
    drain_exchange(line_b, 1, lines)
    write(pl.ds(0, early), 0).wait()
    write(pl.ds(early, LAST), 1).wait()


def hand_out(early, found_ref, centre_ref, spread_ref, coh_ref):
    centre_ref[...] = found_ref[0:3, :]
    spread_ref[...] = found_ref[3:6, :]
    row = found_ref[6:7, early : early + LAST]
    lane = lax.broadcasted_iota(jnp.int32, (1, LAST), 1)
    for direction in range(3):
        coh_ref[direction] = jnp.sum(jnp.where(lane == direction, row, 0.0))


def solution(mesh):
    nx, ny, nz = mesh.shape["kx"], mesh.shape["ky"], mesh.shape["kz"]
    levels = nx // 2

    def shards(coefficients, shift_blocks):
        bands, width = coefficients.shape[4], coefficients.shape[5]
        own = coefficients.reshape(2, bands, width)
        sends = bands // SEND_ROWS
        dma = pltpu.SemaphoreType.DMA
        early = bands - LAST
        f32 = jnp.float32
        found = pl.pallas_call(
            functools.partial(kernel, nx, ny, nz),
            out_shape=jax.ShapeDtypeStruct((8, bands), f32),
            in_specs=[
                pl.BlockSpec(memory_space=pl.ANY),
                pl.BlockSpec(memory_space=pl.ANY),
            ],
            out_specs=pl.BlockSpec(memory_space=pl.ANY),
            scratch_shapes=[
                pltpu.SMEM((3,), jnp.int32),
                pltpu.VMEM((8, bands), f32),
                pltpu.VMEM((2, bands, width), jnp.bfloat16),
                pltpu.VMEM((2, bands, width), jnp.bfloat16),
                pltpu.VMEM((3, 2, width, bands), jnp.bfloat16),
                pltpu.VMEM((3, 2, bands, width), jnp.bfloat16),
                pltpu.VMEM((8, bands), f32),
                pltpu.VMEM((8, bands), f32),
                pltpu.VMEM((3, 8, HALF), f32),
                pltpu.VMEM((8, 4, early), f32),
                pltpu.VMEM((nz, 8, early), f32),
                pltpu.VMEM((levels, 8, early), f32),
                pltpu.VMEM((nz, 8, 4, LAST), f32),
                pltpu.VMEM((levels, 8, LAST), f32),
                dma(()), dma((2,)), dma((2,)),
                dma((sends,)), dma((sends,)), dma((sends,)), dma((sends,)),
                dma((3, sends)),
                dma((1, 8)), dma((1, 8)),
                dma((1, nz)), dma((1, nz)),
                dma((2, levels)), dma((2, levels)),
                dma((8 * nz,)), dma((nz, 8)),
                pltpu.SemaphoreType.REGULAR, pltpu.SemaphoreType.REGULAR,
            ],
            compiler_params=pltpu.CompilerParams(
                collective_id=0,
                has_side_effects=True,
                vmem_limit_bytes=60 * 1024 * 1024,
            ),
        )(shift_blocks, own)
        centre, spread, coherence = pl.pallas_call(
            functools.partial(hand_out, early),
            out_shape=(
                jax.ShapeDtypeStruct((3, bands), f32),
                jax.ShapeDtypeStruct((3, bands), f32),
                jax.ShapeDtypeStruct((3,), f32),
            ),
            out_specs=(
                pl.BlockSpec(memory_space=pltpu.VMEM),
                pl.BlockSpec(memory_space=pltpu.VMEM),
                pl.BlockSpec(memory_space=pltpu.SMEM),
            ),
        )(found)
        return centre, spread, coherence.reshape(3, 1, 1, 1)

    return jax.shard_map(
        shards,
        mesh=mesh,
        in_specs=(P(None, "kx", "ky", "kz", None, None), P()),
        out_specs=(P(), P(), P(None, "kx", "ky", "kz")),
        check_vma=False,
    )
```

time: 87.9 us -> 79.9 us (0.909)
  Pallas kernels: 84.3 us -> 79.1 us
  local copies, waits for them, and re-layouts: 2.7 us -> 0 us
    pallas_call x1 -> x2, Pallas kernels: 84.3 us -> 79.1 us  [the longest x1 77.7 us: shards(): pl.pallas_call(functools.partial(kernel, nx, ny, nz), out_shape=jax.Shape...]
    slice x2 -> x0, local copies, waits for them, and re-layouts: 2.7 us -> none  [shards(): return (out[0:3], out[3:6], coherence[:, 0:1].reshape(3, 1, 1, 1))]
where the time goes in v2:
time: 79.9 us; the launch traced here: 79.7 us
  Pallas kernels  79.1 us (99%)
    pallas_call x1, Pallas kernels, shards(): pl.pallas_call(functools.partial(kernel, nx, ny, nz), out_shape=jax.Shape...  77.7 us

profile of v2, /device:TPU:1, one launch (start us, length us, event | category | flops | bytes accessed | tf_op | source)
XLA Modules:
  0.0 79.7 jit_solution(14568227370744268403)
XLA Ops:
  0.6 77.7 %shard_map.49.found_ref = f32[8,512]{1,0:T(8,128)} custom-call(s32[3]{0:T(128)} %shift_hbm.1, bf16[2,512,2048]{2,1,0:T(8,128)(2,1)} %bitcast.2), custom_call_target="tpu_custom_call" | custom-call | tf_op jit(solution)/shard_map/pallas_call | solution.py:506
  78.4 1.4 %shard_map.50 = (f32[3,512]{1,0:T(4,128)}, f32[3,512]{1,0:T(4,128)}, f32[3]{0:T(128)}) custom-call(f32[8,512]{1,0:T(8,128)} %shard_map.49.found_ref), custom_call_target="tpu_custom_call" | custom-call | tf_op jit(solution)/shard_map/pallas_call | solution.py:544

commit v3 on v2

--- a/solution.py
+++ b/solution.py
@@ -21,12 +21,11 @@
 
 def kernel(
     nx, ny, nz,
-    shift_hbm, c_ref, out_ref,
-    shift_ref, result, own, turned, left, got, dre, dim, squares,
+    shift_hbm, c_ref, result,
+    shift_ref, own, turned, left, got, dre, dim, squares,
     plane_a, column_a, line_a, sheet_b, line_b,
-    shift_sem, own_sem, out_sem, send_a, send_y, send_fx, send_fz, recv,
-    plane_send, plane_recv, column_send, column_recv, line_send, line_recv,
-    sheet_send, sheet_recv,
+    shift_sem, own_sem, send_a, send_y, send_fx, send_fz, first_recv, later_recv,
+    group_sems,
     second_ring, third_ring,
 ):
     kx, ky, kz = lax.axis_index("kx"), lax.axis_index("ky"), lax.axis_index("kz")
@@ -83,12 +82,12 @@
     def rows_of(index):
         return pl.ds(pl.multiple_of(index * SEND_ROWS, SEND_ROWS), SEND_ROWS)
 
-    def remote(source, target_slot, index, send, target):
+    def remote(source, target_slot, rows, send, receive, target):
         return pltpu.make_async_remote_copy(
-            src_ref=source.at[:, rows_of(index), :],
-            dst_ref=got.at[target_slot, :, rows_of(index), :],
-            send_sem=send.at[index],
-            recv_sem=recv.at[target_slot, index],
+            src_ref=source.at[:, rows, :],
+            dst_ref=got.at[target_slot, :, rows, :],
+            send_sem=send,
+            recv_sem=receive,
             device_id=target,
             device_id_type=MESH,
         )
@@ -101,26 +100,33 @@
     cross = device(other_x, 3 - ky, kz)
     along = device((kx + jnp.where(xl == 0, 2, nx - 2)) % nx, ky, kz)
 
+    first = device(first_x, first_y, kz)
+    string = device(kx, string_y, string_z)
+
     def to_first(index):
-        return remote(own, 0, index, send_a, device(first_x, first_y, kz))
+        return remote(own, 0, rows_of(index), send_a, first_recv.at[index], first)
 
     def to_string(index):
-        return remote(own, string_slot, index, send_y, device(kx, string_y, string_z))
+        receive = later_recv.at[string_slot - 1, index // per_step]
+        return remote(own, string_slot, rows_of(index), send_y, receive, string)
 
     def to_cross(index):
-        return remote(got.at[0], 2, index, send_fx, cross)
+        receive = later_recv.at[1, index // per_step]
+        return remote(got.at[0], 2, rows_of(index), send_fx, receive, cross)
 
     def to_along(index):
-        return remote(got.at[0], 1, index, send_fz, along)
-
-    def arrived(edge, index):
-        return pltpu.make_async_remote_copy(
-            src_ref=got.at[edge, :, rows_of(index), :],
-            dst_ref=got.at[edge, :, rows_of(index), :],
-            send_sem=send_a.at[index],
-            recv_sem=recv.at[edge, index],
-            device_id=cross,
-            device_id_type=MESH,
+        receive = later_recv.at[0, index // per_step]
+        return remote(got.at[0], 1, rows_of(index), send_fz, receive, along)
+
+    def arrived(index):
+        return remote(
+            got.at[0], 0, rows_of(index), send_a, first_recv.at[index], first
+        )
+
+    def step_arrived(edge, step):
+        rows = pl.ds(pl.multiple_of(step * STEP_ROWS, STEP_ROWS), STEP_ROWS)
+        return remote(
+            got.at[0], edge, rows, send_a, later_recv.at[edge - 1, step], first
         )
 
     def start_own(index, carry):
@@ -181,7 +187,7 @@
         lax.fori_loop(piece * share, (piece + 1) * share, body, 0)
 
     def pass_on(index):
-        arrived(0, index).wait_recv()
+        arrived(index).wait_recv()
         to_cross(index).start()
         to_along(index).start()
 
@@ -216,7 +222,7 @@
     @pl.when(jnp.logical_not(active))
     def _():
         def body(index, carry):
-            arrived(0, index).wait_recv()
+            arrived(index).wait_recv()
             return carry
 
         lax.fori_loop(0, sends, body, 0)
@@ -250,37 +256,36 @@
                 jnp.where(on, imag, 0.0), axis=0, keepdims=True
             )
 
-    def copy_of(buffer, part, me, target, count, place, send, receive, step):
+    def copy_of(buffer, where, target, send, receive):
         return pltpu.make_async_remote_copy(
-            src_ref=buffer.at[me],
-            dst_ref=buffer.at[me],
-            send_sem=send.at[part, step],
-            recv_sem=receive.at[part, me],
-            device_id=place(target),
+            src_ref=buffer.at[where],
+            dst_ref=buffer.at[where],
+            send_sem=send,
+            recv_sem=receive,
+            device_id=target,
             device_id_type=MESH,
         )
 
-    planes = (slot, 8, in_plane, plane_send, plane_recv)
-    columns_y = (kz, nz, in_column, column_send, column_recv)
-    lines = (level, levels, in_line, line_send, line_recv)
-
-    def start_exchange(buffer, part, group):
-        me, count, place, send, receive = group
+    def all_of(buffer, count, send, receive):
+        return copy_of(buffer, pl.ds(0, count - 1), first, send, receive)
+
+    plane_sems, column_sems, line_a_sems, line_b_sems, sheet_sems = (
+        (group_sems.at[0, index], group_sems.at[1, index]) for index in range(5)
+    )
+    planes = (slot, 8, in_plane)
+    columns_y = (kz, nz, in_column)
+    lines = (level, levels, in_line)
+
+    def start_exchange(buffer, group, semaphores):
+        me, count, place = group
         for step in range(1, count):
-            target = (me + step) % count
-            copy_of(buffer, part, me, target, count, place, send, receive, step).start()
-
-    def await_exchange(buffer, part, group):
-        me, count, place, send, receive = group
-        for step in range(1, count):
-            other = (me + step) % count
-            copy_of(buffer, part, other, other, count, place, send, receive, step).wait_recv()
-
-    def drain_exchange(buffer, part, group):
-        me, count, place, send, receive = group
-        for step in range(1, count):
-            target = (me + step) % count
-            copy_of(buffer, part, me, target, count, place, send, receive, step).wait_send()
+            copy_of(buffer, me, place((me + step) % count), *semaphores).start()
+
+    def await_exchange(buffer, group, semaphores):
+        all_of(buffer, group[1], *semaphores).wait_recv()
+
+    def drain_exchange(buffer, group, semaphores):
+        all_of(buffer, group[1], *semaphores).wait_send()
 
     def plane_means(plane, column):
         groups = [[], [], []]
@@ -321,34 +326,19 @@
         result[0:3, where] = -count * mean / (2.0 * jnp.pi)
         result[3:6, where] = scale * scale * (spreads / (nx * ny * nz))
 
-    def write(where, index):
-        return pltpu.make_async_copy(
-            result.at[:, where], out_ref.at[:, where], out_sem.at[index]
-        )
-
-    def sheet_copy(plane_at, y_at, place, step):
-        return pltpu.make_async_remote_copy(
-            src_ref=sheet_b.at[y_at, plane_at],
-            dst_ref=sheet_b.at[y_at, plane_at],
-            send_sem=sheet_send.at[step],
-            recv_sem=sheet_recv.at[y_at, plane_at],
-            device_id=place,
-            device_id_type=MESH,
-        )
-
     def sheet_peers():
         for shift in range(nz):
             for step in range(8):
                 if shift or step:
                     to_plane, to_y = (slot + step) % 8, (kz + shift) % nz
                     place = device(2 * level + to_plane // 4, to_plane % 4, to_y)
-                    yield shift * 8 + step, to_plane, to_y, place
+                    yield place
 
     def sheet_means():
         parts = [[], []]
         for y_at in range(nz):
             for index in range(8):
-                parts[index // 4 != index % 2].append(sheet_b[y_at, index, 0:3, :])
+                parts[index // 4 != index % 2].append(sheet_b[y_at * 8 + index, 0:3, :])
         number = float(8 * nz)
         one, two = sum(parts[0]), sum(parts[1])
         means = [
@@ -366,8 +356,7 @@
         line_b[level, 5:6, :] = two[1:2] + two[2:3]
 
     def finish_rows(edge, step, local):
-        for inner in range(per_step):
-            arrived(edge, step * per_step + inner).wait_recv()
+        step_arrived(edge, step).wait_recv()
         product(edge, step, local)
 
     def trip(step, carry):
@@ -395,7 +384,7 @@
         def _():
             phases = lax.atan2(dim[:, 0:early], dre[:, 0:early])
             plane_a[slot, 0:3, :] = phases[0:3]
-            start_exchange(plane_a, 0, planes)
+            start_exchange(plane_a, planes, plane_sems)
 
         maybe_pass(0)
         product(0, step, first_local)
@@ -416,46 +405,40 @@
         total = jnp.sum(squares[edge], keepdims=True) / bands
         found = jnp.where(lane == 3 * slot + edge, total, found)
     phases = lax.atan2(dim[:, early:bands], dre[:, early:bands])
-    sheet_b[kz, slot, 0:3, :] = phases[0:3]
-    sheet_b[kz, slot, 3:4, :] = found
+    sheet_b[kz * 8 + slot, 0:3, :] = phases[0:3]
+    sheet_b[kz * 8 + slot, 3:4, :] = found
     pl.semaphore_wait(third_ring, 2 + len(next_but_one))
-    for step, _, _, place in sheet_peers():
-        sheet_copy(slot, kz, place, step).start()
-
-    await_exchange(plane_a, 0, planes)
+    for place in sheet_peers():
+        copy_of(sheet_b, kz * 8 + slot, place, *sheet_sems).start()
+
+    await_exchange(plane_a, planes, plane_sems)
     plane_means(plane_a, column_a)
-    start_exchange(column_a, 0, columns_y)
-
-    for step, from_plane, from_y, place in sheet_peers():
-        sheet_copy(from_plane, from_y, place, step).wait_recv()
+    start_exchange(column_a, columns_y, column_sems)
+
+    all_of(sheet_b, 8 * nz, *sheet_sems).wait_recv()
     sheet_means()
-    plane_found = sum(sheet_b[kz, index, 3:4, :] for index in range(8))
-    above = sum(sheet_b[up, index, 3:4, :] for index in range(8))
+    plane_found = sum(sheet_b[kz * 8 + index, 3:4, :] for index in range(8))
+    above = sum(sheet_b[up * 8 + index, 3:4, :] for index in range(8))
     line_b[level, 6:7, :] = plane_found
-    start_exchange(line_b, 1, lines)
-
-    await_exchange(column_a, 0, columns_y)
+    start_exchange(line_b, lines, line_b_sems)
+
+    await_exchange(column_a, columns_y, column_sems)
     column_means(column_a, line_a)
-    start_exchange(line_a, 0, lines)
-    drain_exchange(plane_a, 0, planes)
-    drain_exchange(column_a, 0, columns_y)
-    for step, _, _, place in sheet_peers():
-        sheet_copy(slot, kz, place, step).wait_send()
-
-    def finish(index, carry):
-        to_first(index).wait_send()
-        to_string(index).wait_send()
-
-        @pl.when(active)
-        def _():
-            to_cross(index).wait_send()
-            to_along(index).wait_send()
-
-        return carry
-
-    lax.fori_loop(0, sends, finish, 0)
-
-    await_exchange(line_b, 1, lines)
+    start_exchange(line_a, lines, line_a_sems)
+    drain_exchange(plane_a, planes, plane_sems)
+    drain_exchange(column_a, columns_y, column_sems)
+    all_of(sheet_b, 8 * nz, *sheet_sems).wait_send()
+
+    everything = pl.ds(0, bands)
+    remote(own, 0, everything, send_a, own_sem.at[0], first).wait_send()
+    remote(own, string_slot, everything, send_y, own_sem.at[0], string).wait_send()
+
+    @pl.when(active)
+    def _():
+        remote(got.at[0], 2, everything, send_fx, own_sem.at[0], cross).wait_send()
+        remote(got.at[0], 1, everything, send_fz, own_sem.at[0], along).wait_send()
+
+    await_exchange(line_b, lines, line_b_sems)
     results(line_b, slice(early, bands))
     ahead = line_b[(level + 1) % levels, 6:7, :]
     x_from = jnp.where(xl == 0, 3 * (core * 4 + ky), 3 * (core * 4 + ky) + 1)
@@ -473,14 +456,10 @@
         value = jnp.sum(jnp.where(lane == place, row, 0.0), axis=1, keepdims=True)
         coherences = jnp.where(lane == direction, value, coherences)
     result[6:7, early:bands] = coherences
-    write(pl.ds(early, LAST), 1).start()
-    await_exchange(line_a, 0, lines)
+    await_exchange(line_a, lines, line_a_sems)
     results(line_a, slice(0, early))
-    write(pl.ds(0, early), 0).start()
-    drain_exchange(line_a, 0, lines)
-    drain_exchange(line_b, 1, lines)
-    write(pl.ds(0, early), 0).wait()
-    write(pl.ds(early, LAST), 1).wait()
+    drain_exchange(line_a, lines, line_a_sems)
+    drain_exchange(line_b, lines, line_b_sems)
 
 
 def hand_out(early, found_ref, centre_ref, spread_ref, coh_ref):
@@ -507,13 +486,12 @@
             functools.partial(kernel, nx, ny, nz),
             out_shape=jax.ShapeDtypeStruct((8, bands), f32),
             in_specs=[
-                pl.BlockSpec(memory_space=pl.ANY),
-                pl.BlockSpec(memory_space=pl.ANY),
+                pl.BlockSpec(memory_space=pltpu.HBM),
+                pl.BlockSpec(memory_space=pltpu.HBM),
             ],
-            out_specs=pl.BlockSpec(memory_space=pl.ANY),
+            out_specs=pl.BlockSpec(memory_space=pltpu.VMEM),
             scratch_shapes=[
                 pltpu.SMEM((3,), jnp.int32),
-                pltpu.VMEM((8, bands), f32),
                 pltpu.VMEM((2, bands, width), jnp.bfloat16),
                 pltpu.VMEM((2, bands, width), jnp.bfloat16),
                 pltpu.VMEM((3, 2, width, bands), jnp.bfloat16),
@@ -524,21 +502,18 @@
                 pltpu.VMEM((8, 4, early), f32),
                 pltpu.VMEM((nz, 8, early), f32),
                 pltpu.VMEM((levels, 8, early), f32),
-                pltpu.VMEM((nz, 8, 4, LAST), f32),
+                pltpu.VMEM((8 * nz, 4, LAST), f32),
                 pltpu.VMEM((levels, 8, LAST), f32),
-                dma(()), dma((2,)), dma((2,)),
-                dma((sends,)), dma((sends,)), dma((sends,)), dma((sends,)),
-                dma((3, sends)),
-                dma((1, 8)), dma((1, 8)),
-                dma((1, nz)), dma((1, nz)),
-                dma((2, levels)), dma((2, levels)),
-                dma((8 * nz,)), dma((nz, 8)),
+                dma(()), dma((2,)),
+                dma(()), dma(()), dma(()), dma(()),
+                dma((sends,)), dma((2, bands // STEP_ROWS)),
+                dma((2, 5)),
                 pltpu.SemaphoreType.REGULAR, pltpu.SemaphoreType.REGULAR,
             ],
             compiler_params=pltpu.CompilerParams(
                 collective_id=0,
                 has_side_effects=True,
-                vmem_limit_bytes=60 * 1024 * 1024,
+                vmem_limit_bytes=52 * 1024 * 1024,
             ),
         )(shift_blocks, own)
         centre, spread, coherence = pl.pallas_call(
@@ -553,6 +528,7 @@
                 pl.BlockSpec(memory_space=pltpu.VMEM),
                 pl.BlockSpec(memory_space=pltpu.SMEM),
             ),
+            compiler_params=pltpu.CompilerParams(vmem_limit_bytes=2 * 1024 * 1024),
         )(found)
         return centre, spread, coherence.reshape(3, 1, 1, 1)
 

time: 79.9 us -> 76.4 us (0.956)
  Pallas kernels: 79.1 us -> 75 us
    pallas_call x1, Pallas kernels: 77.7 us -> 74.4 us  [shards(): pl.pallas_call(functools.partial(kernel, nx, ny, nz), out_shape=jax.Shape...]
where the time goes in v3:
time: 76.4 us; the launch traced here: 76.3 us
  Pallas kernels  75 us (98%)
    pallas_call x1, Pallas kernels, shards(): pl.pallas_call(functools.partial(kernel, nx, ny, nz), out_shape=jax.Shape...  74.4 us

profile of v3, /device:TPU:1, one launch (start us, length us, event | category | flops | bytes accessed | tf_op | source)
XLA Modules:
  0.0 76.3 jit_solution(14349042919604778075)
XLA Ops:
  0.6 0.0 copy-start
  0.6 0.6 copy-done
  1.3 74.4 %shard_map.49.found_ref = f32[8,512]{1,0:T(8,128)S(1)} custom-call(s32[3]{0:T(128)S(1)} %copy-done, bf16[2,512,2048]{2,1,0:T(8,128)(2,1)} %bitcast.2), custom_call_target="tpu_custom_call" | custom-call | tf_op jit(solution)/shard_map/pallas_call | solution.py:485
  75.7 0.6 shard_map.50
Async XLA Ops:
  0.6 0.7 copy-start
